TPU v7x, 512 devices: a whole 4x8x8 slice. The times are simulated.
512 devices in a mesh: space: 64 (over z, y_lo, x), mode: 8 (over y_hi, core).
Axes of the slice: x: 4, y: 8 (y_hi: 4, y_lo: 2; y = y_hi * 2 + y_lo), z: 8, core: 2. Of those that a mesh axis runs over, the one named last changes fastest.
Arguments:
- modes: float32 [3, 128, 65536], P(None, 'mode', 'space'), may hold values from -16 to 16
- stencil_coef: float32 [3, 6, 65536], P(None, None, 'space'), may hold values from -3 to 3
- volumes: float32 [65536], P('space'), may hold values from 0.5 to 2
- neighbours: int32 [6, 65536], P(None, 'space'), may hold values from 0 to 65535, as said below
Outputs:
- tensor: float32 [128, 128, 128], P('mode', 'space')
Inputs may be any that keep to these rules, and one draw needn't show every extreme that they name: `neighbours`: each entry differs from its own cell's index by 1 to 128.
All inputs are finite; a program needn't handle non-finite values.
Results may differ from a plain program's by a relative error of at most 0.005.
Values may be sent and summed in bfloat16 or wider, within the bound.
No kernel may reach another device: no remote copies, remote signals or barrier semaphores. Data moves between devices by JAX's collectives and lax.ppermute only.
A program may use at most 64 MiB of HBM per device.

v0:
```python
import math

import jax
import jax.numpy as jnp
from jax import lax
from jax.sharding import PartitionSpec as P


def sent_to_all(shard, axis):
    copies = jnp.broadcast_to(shard, (lax.axis_size(axis), *shard.shape))
    return lax.all_to_all(copies, axis, split_axis=0, concat_axis=0, tiled=True)


def laid_out(tiles, dim):
    tiles = jnp.moveaxis(tiles, 0, dim)
    lengths = tiles.shape
    return tiles.reshape(*lengths[:dim], lengths[dim] * lengths[dim + 1], *lengths[dim + 2 :])


def gathered_copies(shard, axis, dim):
    tiles = sent_to_all(shard, axis)
    return laid_out(tiles, dim)


def with_halo(cells, sides, width):
    for axis, dim in sides:
        count = lax.axis_size(axis)
        ends = count - 1
        head = lax.slice_in_dim(cells, 0, width, axis=dim)
        tail = lax.slice_in_dim(cells, cells.shape[dim] - width, cells.shape[dim], axis=dim)
        cells = jnp.concatenate(
            [
                lax.ppermute(tail, axis, [(i, (i + 1) % count) for i in range(ends)]),
                cells,
                lax.ppermute(head, axis, [((i + 1) % count, i) for i in range(ends)]),
            ],
            axis=dim,
        )
    return cells


def cut_along(shard, dim, length):
    before, after = (shard.shape[:dim], shard.shape[dim + 1 :])
    return jnp.moveaxis(shard.reshape(*before, length, -1, *after), dim, 0)


def summed_on_arrival(shard, axis, dim):
    length = lax.axis_size(axis)
    tiles = lax.all_to_all(cut_along(shard, dim, length), axis, 0, 0, tiled=True)
    return jnp.sum(tiles, axis=0)


def local_term(modes, stencil_coef, volumes, neighbours):
    width = modes.shape[2]
    count_local = modes.shape[1]
    reach = width // 8
    extended = width + 2 * reach
    scale = 1.0 / math.sqrt(width * lax.axis_size("space"))
    low_local = modes.astype(jnp.bfloat16)
    low = gathered_copies(low_local, "mode", 1)
    padded = with_halo(modes, (("space", 2),), reach)
    offset = lax.axis_index("space") * width - reach
    local_index = neighbours - offset
    columns = jnp.arange(extended, dtype=jnp.int32)
    cell_place = jnp.arange(width, dtype=jnp.int32)
    centre_hit = (columns[None, :] == cell_place[:, None] + reach).astype(jnp.float32)
    band = jnp.zeros((3, width, extended), jnp.float32)
    coef_total = jnp.zeros((3, width), jnp.float32)
    for step in range(stencil_coef.shape[1]):
        hit = (local_index[step][:, None] == columns[None, :]).astype(jnp.float32)
        band = band + stencil_coef[:, step][:, :, None] * hit[None]
        coef_total = coef_total + stencil_coef[:, step]
    band = band - coef_total[:, :, None] * centre_hit[None]
    grads = jnp.einsum(
        "dxy,cky->dckx",
        band,
        padded,
        precision=lax.Precision.HIGHEST,
        preferred_element_type=jnp.float32,
    )
    weight = volumes * scale
    low_wide = low.astype(jnp.float32)
    mixed = grads[0][:, :, None, :] * low_wide[0][None, None]
    mixed = mixed + grads[1][:, :, None, :] * low_wide[1][None, None]
    mixed = mixed + grads[2][:, :, None, :] * low_wide[2][None, None]
    carried = (mixed * weight[None, None, None, :]).astype(jnp.bfloat16)
    total_modes = low.shape[1]
    carried_flat = jnp.transpose(carried, (1, 2, 0, 3)).reshape(
        count_local * total_modes, 3 * width
    )
    low_flat = jnp.transpose(low, (1, 0, 2)).reshape(total_modes, 3 * width)
    product = lax.dot_general(
        low_flat, carried_flat, (((1,), (1,)), ((), ())), preferred_element_type=jnp.float32
    )
    return jnp.transpose(product.reshape(total_modes, count_local, total_modes), (1, 0, 2))


def body(modes, stencil_coef, volumes, neighbours):
    full_term = local_term(modes, stencil_coef, volumes, neighbours)
    shares = summed_on_arrival(full_term, "space", 1)
    return shares


def solution(mesh):
    in_specs = (P(None, "mode", "space"), P(None, None, "space"), P("space"), P(None, "space"))
    out_specs = P("mode", "space", None)
    return jax.shard_map(body, mesh=mesh, in_specs=in_specs, out_specs=out_specs, check_vma=False)
```

profile of v0, /device:TPU:40, one launch (start us, length us, event | category | flops | bytes accessed | tf_op | source)
XLA Modules:
  0.0 147.2 jit_solution(2536061459543058233)
XLA Ops:
  0.0 1.4 fusion.47
  1.4 3.4 %collective-permute-start = (f32[3,16,128]{2,1,0:T(8,128)}, f32[3,16,128]{2,1,0:T(8,128)}, u32[]{:S(2)}, u32[]{:S(2)}) collective-permute-start(f32[3,16,128]{2,1,0:T(8,128)} %get-tuple-element.11), channel_id=1, source_target_pairs={{0,8},{8,16},{16,24},{24,32},{32,40},{40,48},{48,56},{56,64},{64,7... | collective-permute-start | bytes 73736 | tf_op jit(solution)/shard_map/ppermute | solution.py:33
  4.8 4.6 %collective-permute-start.1 = (f32[3,16,128]{2,1,0:T(8,128)}, f32[3,16,128]{2,1,0:T(8,128)}, u32[]{:S(2)}, u32[]{:S(2)}) collective-permute-start(f32[3,16,128]{2,1,0:T(8,128)} %get-tuple-element.12), channel_id=1, source_target_pairs={{8,0},{16,8},{24,16},{32,24},{40,32},{48,40},{56,48},{64,56},{72,6... | collective-permute-start | bytes 73736 | tf_op jit(solution)/shard_map/ppermute | solution.py:35
  9.3 0.9 convert_element_type.76
  10.3 1.0 broadcast_in_dim.2
  11.3 7.2 %all-to-all-start = ((bf16[8,3,16,1024]{3,2,1,0:T(8,128)(2,1)}), bf16[8,3,16,1024]{3,2,1,0:T(8,128)(2,1)}, u32[]{:S(2)}, u32[]{:S(2)}) async-start(bf16[8,3,16,1024]{3,2,1,0:T(8,128)(2,1)} %broadcast_in_dim.2), calls=%async_computation | async-start | bytes 1572864 | tf_op jit(solution)/shard_map/all_to_all | solution.py:11
  18.5 1.4 fusion.48
  19.9 0.6 copy_bitcast_fusion.2
  20.5 0.6 add_add_fusion
  21.1 0.6 copy_bitcast_fusion.4
  21.7 0.8 broadcast_subtract_fusion
  22.5 0.4 fusion.38
  22.9 1.3 fusion.32
  24.3 3.0 %fusion.34 = (f32[1024,1280]{1,0:T(8,128)S(1)}, f32[1024,1280]{1,0:T(8,128)}) fusion(s32[1024]{0:T(1024)S(1)} %bitcast.91, s32[1024]{0:T(1024)S(1)} %bitcast.90), kind=kLoop, calls=%fused_computation.42 | loop fusion | flops 5242880 | bytes 10493952 | tf_op jit(solution)/shard_map/convert_element_type | solution.py:70
  27.2 4.7 %fusion.36 = (f32[1024,1280]{1,0:T(8,128)}, f32[1024,1280]{1,0:T(8,128)}) fusion(s32[1024]{0:T(1024)S(1)} %bitcast.89, s32[1024]{0:T(1024)S(1)} %bitcast.88), kind=kLoop, calls=%fused_computation.44 | loop fusion | flops 5242880 | bytes 10493952 | tf_op jit(solution)/shard_map/convert_element_type | solution.py:70
  31.9 28.7 %fusion.39 = f32[3,3,16,1024]{3,2,0,1:T(8,128)} fusion(f32[1024,1280]{1,0:T(8,128)S(1)} %fusion.38, f32[3,1024]{1,0:T(4,128)} %add_add_fusion, f32[1024,1280]{1,0:T(8,128)} %get-tuple-element.36, f32[3,1024]{1,0:T(4,128)S(1)} %get-tuple-element.25, f32[1024,1280]{1,0:T(8,128)} %get-tuple-element.35, f32[3,1024]{1,0:T(4,128)S(1)} %get-tuple-element.26, ...), kind=kOutput, calls=%fused_computation.47 | convolution fusion | flops 2316165120 | bytes 37621760 | tf_op jit(solution)/shard_map/dxy,cky->dckx/dot_general | solution.py:74
  60.6 1.2 slice_bitcast_fusion.5
  61.8 0.5 copy.41
  62.2 1.6 %copy.44 = f32[16,3,1024]{0,2,1:T(8,128)} copy(f32[16,3,1024]{2,0,1:T(8,128)S(1)} %get-tuple-element.10) | data formatting | bytes 393216 | tf_op jit(solution)/shard_map/mul | solution.py:84
  63.9 1.6 %copy.46 = f32[16,3,1024]{0,2,1:T(8,128)} copy(f32[16,3,1024]{2,0,1:T(8,128)S(1)} %get-tuple-element.9) | data formatting | bytes 393216 | tf_op jit(solution)/shard_map/mul | solution.py:85
  65.5 1.2 copy.42
  66.7 0.2 bitcast_convert_fusion
  66.9 1.1 slice_bitcast_fusion.2
  68.0 0.2 copy.43
  68.2 1.2 copy.45
  69.5 2.0 %copy.47 = f32[128,1024]{0,1:T(8,128)} copy(f32[128,1024]{1,0:T(8,128)} %get-tuple-element.6) | data formatting | bytes 1048576 | tf_op jit(solution)/shard_map/mul | solution.py:85
  71.5 1.2 copy.48
  72.7 25.1 %multiply_convert_fusion = bf16[16,128,3,1024]{1,0,3,2:T(8,128)(2,1)S(1)} fusion(f32[1024]{0:T(1024)S(1)} %broadcast_multiply_fusion, f32[128,1024]{0,1:T(8,128)} %copy.47, f32[16,3,1024]{0,2,1:T(8,128)} %copy.46, f32[128,1024]{0,1:T(8,128)S(1)} %copy.45, f32[16,3,1024]{0,2,1:T(8,128)} %copy.44, f32[128,1024]{0,1:T(8,128)S(1)} %copy.43, f32[16,3,1024]{0,2,1:T(8,128)S(1)} %copy.41), kind=kLoop, calls=%fused_computation | loop fusion | flops 44040192 | bytes 14749696 | tf_op jit(solution)/shard_map/convert_element_type | solution.py:86
  97.8 5.3 %fusion.15 = f32[2048,128]{1,0:T(8,128)S(1)} fusion(bf16[128,3072]{0,1:T(8,128)(2,1)S(1)} %bitcast.87, bf16[384,8,16,128]{3,2,1,0:T(8,128)(2,1)S(1)} %bitcast.83), kind=kOutput, calls=%fused_computation.16 | convolution fusion | flops 1610612736 | bytes 14417920 | tf_op jit(solution)/shard_map/dot_general | solution.py:92
  103.1 0.5 copy.49
  103.6 42.9 %all_to_all.10 = f32[64,16,2,128]{3,1,2,0:T(8,128)S(1)} all-to-all(f32[64,16,2,128]{3,1,2,0:T(8,128)S(1)} %bitcast.85), channel_id=1, replica_groups=mesh['space'=64,'mode'=8] {'space'}, dimensions={0} | all-to-all | bytes 2097152 | tf_op jit(solution)/shard_map/all_to_all | solution.py:49
  146.6 0.6 copy.50
  (12 shorter events, 0.1 us)
Async XLA Ops:
  1.4 30.6 %collective-permute-start = (f32[3,16,128]{2,1,0:T(8,128)}, f32[3,16,128]{2,1,0:T(8,128)}, u32[]{:S(2)}, u32[]{:S(2)}) collective-permute-start(f32[3,16,128]{2,1,0:T(8,128)} %get-tuple-element.11), channel_id=1, source_target_pairs={{0,8},{8,16},{16,24},{24,32},{32,40},{40,48},{48,56},{56,64},{64,7... | collective-permute-start | bytes 73736 | tf_op jit(solution)/shard_map/ppermute | solution.py:33
  4.8 27.2 %collective-permute-start.1 = (f32[3,16,128]{2,1,0:T(8,128)}, f32[3,16,128]{2,1,0:T(8,128)}, u32[]{:S(2)}, u32[]{:S(2)}) collective-permute-start(f32[3,16,128]{2,1,0:T(8,128)} %get-tuple-element.12), channel_id=1, source_target_pairs={{8,0},{16,8},{24,16},{32,24},{40,32},{48,40},{56,48},{64,56},{72,6... | collective-permute-start | bytes 73736 | tf_op jit(solution)/shard_map/ppermute | solution.py:35
  11.3 54.2 %all-to-all-start = ((bf16[8,3,16,1024]{3,2,1,0:T(8,128)(2,1)}), bf16[8,3,16,1024]{3,2,1,0:T(8,128)(2,1)}, u32[]{:S(2)}, u32[]{:S(2)}) async-start(bf16[8,3,16,1024]{3,2,1,0:T(8,128)(2,1)} %broadcast_in_dim.2), calls=%async_computation | async-start | bytes 1572864 | tf_op jit(solution)/shard_map/all_to_all | solution.py:11
  27.2 4.7 %copy-start.1 = (f32[1024]{0:T(1024)S(1)}, f32[1024]{0:T(1024)}, u32[]{:S(2)}) copy-start(f32[1024]{0:T(1024)} %param.6) | copy-start | bytes 12292
  72.7 25.1 %copy-start = (bf16[128,3,1024]{0,2,1:T(8,128)(2,1)S(1)}, bf16[128,3,1024]{0,2,1:T(8,128)(2,1)}, u32[]{:S(2)}) copy-start(bf16[128,3,1024]{0,2,1:T(8,128)(2,1)} %copy.48) | copy-start | bytes 2359300
where the time goes:
time: 148 us; the launch traced here: 147 us
  blocking collectives  42.9 us (29%)
  other arithmetic  37.1 us (25%)
  matrix products  33.9 us (23%)
  local copies, waits for them, and re-layouts  18 us (12%)
  starting transfers between devices  15.1 us (10%)
    all_to_all x1, blocking collectives, summed_on_arrival(): lax.all_to_all(cut_along(shard, dim, length), axis, 0, 0, tiled=True)  42.9 us
    dot_general x1, matrix products, local_term(): jnp.einsum('dxy,cky->dckx', band, padded, precision=lax.Precision.HIGHEST...  28.7 us
    convert_element_type x1, other arithmetic, local_term(): carried = (mixed * weight[None, None, None, :]).astype(jnp.bfloat16)  25.1 us
    convert_element_type x3, other arithmetic, local_term(): hit = (local_index[step][:, None] == columns[None, :]).astype(jnp.float32)  8.98 us
    all_to_all x1, starting transfers between devices, sent_to_all(): return lax.all_to_all(copies, axis, split_axis=0, concat_axis=0, tiled=True)  7.21 us
    dot_general x1, matrix products, local_term(): lax.dot_general(low_flat, carried_flat, (((1,), (1,)), ((), ())), preferr...  5.27 us
    ppermute x1, starting transfers between devices, with_halo(): lax.ppermute(head, axis, [((i + 1) % count, i) for i in range(ends)])  4.55 us
    mul x2, local copies, waits for them, and re-layouts, local_term(): mixed = mixed + grads[2][:, :, None, :] * low_wide[2][None, None]  3.69 us
  transfers between devices with their start and end apart: 3, of which 0 were waited for; matrix products, arithmetic and copies ran while one was open for 33% of the time, Pallas kernels for 0%

commit v1 on v0

v1 whole, which is shorter than its diff:
```python
import math

import jax
import jax.numpy as jnp
from jax import lax
from jax.experimental import pallas as pl
from jax.experimental.pallas import tpu as pltpu
from jax.sharding import Mesh, PartitionSpec as P

SPACE = ("z", "ylo", "x")
MODE = ("yhi", "core")
PLANE = ("ylo", "x")
GROUP = 4
LANES = 128
TILE = 32


def picked(block, lane):
    return jnp.take_along_axis(block, lane, axis=1, mode="promise_in_bounds")


def grads_kernel(scale, near_ref, coef_ref, vol_ref, left_ref, mid_ref, right_ref, out_ref):
    comps, count, width = mid_ref.shape
    dirs, steps = coef_ref.shape[:2]
    tiles = width // LANES
    for t in range(tiles):
        at = slice(t * LANES, (t + 1) * LANES)
        weight = vol_ref[:, at] * scale
        lanes, ahead, behind, coefs = [], [], [], []
        for n in range(steps):
            index = jnp.broadcast_to(near_ref[n : n + 1, at], (8, LANES))
            lanes.append(index & (LANES - 1))
            apart = ((index >> 7) - t) & 3
            ahead.append(apart == 1)
            behind.append(apart == 3)
            coefs.append(
                [jnp.broadcast_to(coef_ref[d, n : n + 1, at] * weight, (8, LANES)) for d in range(dirs)]
            )
        for c in range(comps):
            for r in range(0, count, 8):
                rows = slice(r, r + 8)
                here = mid_ref[c, rows, at]
                if t == 0:
                    before = left_ref[c, rows, :]
                else:
                    before = mid_ref[c, rows, (t - 1) * LANES : t * LANES]
                if t == tiles - 1:
                    after = right_ref[c, rows, :]
                else:
                    after = mid_ref[c, rows, (t + 1) * LANES : (t + 2) * LANES]
                total = [None] * dirs
                for n in range(steps):
                    near = jnp.where(
                        ahead[n],
                        picked(after, lanes[n]),
                        jnp.where(behind[n], picked(before, lanes[n]), picked(here, lanes[n])),
                    )
                    change = near - here
                    for d in range(dirs):
                        term = coefs[n][d] * change
                        total[d] = term if total[d] is None else total[d] + term
                for d in range(dirs):
                    out_ref[pl.ds((d * comps + c) * count + r, 8), at] = total[d]


def weighted_grads(modes, left, right, stencil_coef, volumes, neighbours, scale):
    comps, count, width = modes.shape
    return pl.pallas_call(
        lambda *refs: grads_kernel(scale, *refs),
        out_shape=jax.ShapeDtypeStruct((9 * count, width), jnp.float32),
        in_specs=[pl.BlockSpec(memory_space=pltpu.VMEM)] * 6,
        out_specs=pl.BlockSpec(memory_space=pltpu.VMEM),
        compiler_params=pltpu.CompilerParams(vmem_limit_bytes=4 << 20),
        cost_estimate=pl.CostEstimate(flops=8_000_000, bytes_accessed=1_000_000, transcendentals=0),
        name="grads",
    )(neighbours, stencil_coef, volumes.reshape(1, width), left, modes, right)


def tensor_kernel(grad_ref, own_ref, other_ref, out_ref, wide_ref, flat_ref, held_a, held_b, rows_ref):
    chips, comps, count, width = own_ref.shape
    blocks = 2 * chips
    total = blocks * count
    core = lax.axis_index("core")
    for c in range(comps):
        for h, ref in ((0, own_ref), (1, other_ref)):
            place = core if h == 0 else 1 - core
            for y in range(chips):
                row = pl.multiple_of((2 * y + place) * count, count)
                piece = ref[y, c]
                flat_ref[pl.ds(row, count), pl.ds(c * width, width)] = piece
                wide_ref[c, pl.ds(row, count), :] = piece.astype(jnp.float32)

    def build(group, held):
        for x in range(0, width, LANES):
            at = slice(x, x + LANES)
            for j in range(0, total, TILE):
                low = [wide_ref[d, j : j + TILE, at] for d in range(3)]
                for kk in range(GROUP):
                    k = group * GROUP + kk
                    for c in range(comps):
                        row = [grad_ref[pl.ds((d * comps + c) * count + k, 1), at] for d in range(3)]
                        mixed = low[0] * row[0] + low[1] * row[1] + low[2] * row[2]
                        held[kk * total + j : kk * total + j + TILE, c * width + x : c * width + x + LANES] = (
                            mixed.astype(jnp.bfloat16)
                        )

    def contract(group, held):
        part = lax.dot_general(
            held[...], flat_ref[...], (((1,), (1,)), ((), ())), preferred_element_type=jnp.float32
        )
        for kk in range(GROUP):
            k = group * GROUP + kk
            rows_ref[pl.ds(k, total, stride=count), :] = part[kk * total : (kk + 1) * total].T

    groups = count // GROUP
    helds = (held_a, held_b)
    build(0, helds[0])
    for g in range(groups):
        if g + 1 < groups:
            build(g + 1, helds[(g + 1) % 2])
        contract(g, helds[g % 2])
    first, second, size = out_ref.shape[:3]
    for a in range(first):
        for b in range(second):
            out_ref[a, b] = rows_ref[pl.ds((b * first + a) * size, size), :].astype(jnp.bfloat16)


def local_tensor(grads, own, other, plane, depth):
    chips, comps, count, width = own.shape
    total = 2 * chips * count
    rows = 2 * count
    return pl.pallas_call(
        tensor_kernel,
        out_shape=jax.ShapeDtypeStruct((plane, depth, rows, total), jnp.bfloat16),
        in_specs=[pl.BlockSpec(memory_space=pltpu.VMEM)] * 3,
        out_specs=pl.BlockSpec(memory_space=pltpu.VMEM),
        scratch_shapes=[
            pltpu.VMEM((comps, total, width), jnp.float32),
            pltpu.VMEM((total, comps * width), jnp.bfloat16),
            pltpu.VMEM((GROUP * total, comps * width), jnp.bfloat16),
            pltpu.VMEM((GROUP * total, comps * width), jnp.bfloat16),
            pltpu.VMEM((count * total, total), jnp.float32),
        ],
        compiler_params=pltpu.CompilerParams(vmem_limit_bytes=16 << 20),
        cost_estimate=pl.CostEstimate(flops=1_700_000_000, bytes_accessed=2_000_000, transcendentals=0),
        name="tensor",
    )(grads, own, other)


def sum_kernel(tiles_ref, out_ref):
    total = tiles_ref[0].astype(jnp.float32)
    for i in range(1, tiles_ref.shape[0]):
        total = total + tiles_ref[i].astype(jnp.float32)
    out_ref[...] = total.astype(out_ref.dtype)


def summed(tiles, dtype):
    return pl.pallas_call(
        sum_kernel,
        out_shape=jax.ShapeDtypeStruct(tiles.shape[1:], dtype),
        in_specs=[pl.BlockSpec(memory_space=pltpu.VMEM)],
        out_specs=pl.BlockSpec(memory_space=pltpu.VMEM),
        compiler_params=pltpu.CompilerParams(vmem_limit_bytes=4 << 20),
        cost_estimate=pl.CostEstimate(flops=300_000, bytes_accessed=600_000, transcendentals=0),
        name="summed",
    )(tiles)


def body(modes, stencil_coef, volumes, neighbours):
    comps, count, width = modes.shape
    cells = width * lax.axis_size(SPACE)
    low = modes.astype(jnp.bfloat16)
    chips = lax.axis_size("yhi")
    copies = jnp.broadcast_to(low, (chips, *low.shape))
    own = lax.all_to_all(copies, "yhi", 0, 0, tiled=True)
    last = lax.axis_size(SPACE) - 1
    left = lax.ppermute(modes[:, :, width - LANES :], SPACE, [(i, i + 1) for i in range(last)])
    right = lax.ppermute(modes[:, :, :LANES], SPACE, [(i + 1, i) for i in range(last)])
    grads = weighted_grads(modes, left, right, stencil_coef, volumes, neighbours, 1.0 / math.sqrt(cells))
    other = lax.ppermute(own, "core", [(0, 1), (1, 0)])
    plane, depth = lax.axis_size(PLANE), lax.axis_size("z")
    share = local_tensor(grads, own, other, plane, depth)
    first = lax.all_to_all(share, PLANE, 0, 0, tiled=True)
    partial = summed(first, jnp.bfloat16)
    second = lax.all_to_all(partial, "z", 0, 0, tiled=True)
    rows = summed(second, jnp.float32)
    return jnp.transpose(rows.reshape(2, count, -1), (1, 0, 2))


def solution(mesh):
    sizes = (8, 2, 4, 4, 2)
    fine = Mesh(mesh.devices.reshape(sizes), SPACE + MODE)
    in_specs = (P(None, MODE, SPACE), P(None, None, SPACE), P(SPACE), P(None, SPACE))
    out_specs = P(MODE, SPACE, None)
    return jax.shard_map(body, mesh=fine, in_specs=in_specs, out_specs=out_specs, check_vma=False)
```

time: 148 us -> 78.8 us (0.53)
  the two profiles are of different devices: /device:TPU:40 before, /device:TPU:16 now
where the time goes in v1:
time: 78.8 us; the launch traced here: 78.5 us
  blocking collectives  56.5 us (72%)
  Pallas kernels  10.9 us (14%)
  starting transfers between devices  7.88 us (10%)
  waiting for transfers between devices  1.5 us (2%)
  other arithmetic  0.94 us (1%)
    all_to_all x1, blocking collectives, body(): second = lax.all_to_all(partial, 'z', 0, 0, tiled=True)  20 us
    all_to_all x1, blocking collectives, body(): own = lax.all_to_all(copies, 'yhi', 0, 0, tiled=True)  19.5 us
    all_to_all x1, blocking collectives, body(): first = lax.all_to_all(share, PLANE, 0, 0, tiled=True)  17 us
    pallas_call x1, Pallas kernels, local_tensor(): pl.pallas_call(tensor_kernel, out_shape=jax.ShapeDtypeStruct((plane, dept...  8.91 us
    ppermute x1, starting transfers between devices, body(): lax.ppermute(modes[:, :, width - LANES:], SPACE, [(i, i + 1) for i in ran...  4.55 us
    ppermute x1, starting transfers between devices, body(): other = lax.ppermute(own, 'core', [(0, 1), (1, 0)])  2.04 us
    pallas_call x1, Pallas kernels, weighted_grads(): pl.pallas_call(lambda *refs: grads_kernel(scale, *refs), out_shape=jax.Sh...  1.89 us
  transfers between devices with their start and end apart: 3, of which 1 were waited for; matrix products, arithmetic and copies ran while one was open for 0% of the time, Pallas kernels for 2%

profile of v1, /device:TPU:16, one launch (start us, length us, event | category | flops | bytes accessed | tf_op | source)
XLA Modules:
  0.0 78.5 jit_solution(17468515495474103664)
XLA Ops:
  0.0 0.9 %convert_element_type.3 = bf16[3,16,1024]{2,1,0:T(8,128)(2,1)S(1)} convert(f32[3,16,1024]{2,1,0:T(8,128)} %refs_4_.1) | non-fusion elementwise | flops 49152 | bytes 294912 | tf_op jit(solution)/shard_map/convert_element_type | solution.py:172
  1.0 0.0 copy-start
  1.0 0.0 copy-start.2
  1.0 19.5 %all_to_all.15.own_ref = bf16[4,3,16,1024]{3,2,1,0:T(8,128)(2,1)S(1)} all-to-all(bf16[4,3,16,1024]{3,2,1,0:T(8,128)(2,1)S(1)} %broadcast_in_dim.3), channel_id=1, replica_groups=mesh['z'=8,'ylo'=2,'x'=4,'yhi'=4,'core'=2] {'yhi'}, dimensions={0} | all-to-all | bytes 786432 | tf_op jit(solution)/shard_map/all_to_all | solution.py:175
  20.5 0.0 copy-start.1
  20.5 2.0 %collective-permute-start.2 = (bf16[4,3,16,1024]{3,2,1,0:T(8,128)(2,1)S(1)}, bf16[4,3,16,1024]{3,2,1,0:T(8,128)(2,1)S(1)}, u32[]{:S(2)}, u32[]{:S(2)}) collective-permute-start(bf16[4,3,16,1024]{3,2,1,0:T(8,128)(2,1)S(1)} %all_to_all.15.own_ref), channel_id=1, source_target_pairs={{0,1},{1,0},{2,3},{3,2},{4,5},{5,4},{6,7},{7,6},{8,9},{9,8},{10,11... | collective-permute-start | bytes 1179656 | tf_op jit(solution)/shard_map/ppermute | solution.py:180
  22.5 0.0 copy-done
  22.6 0.0 copy-start.3
  22.6 1.3 %collective-permute-start.1 = (f32[3,16,128]{2,1,0:T(8,128)S(1)}, f32[3,16,128]{2,1,0:T(8,128)S(1)}, u32[]{:S(2)}, u32[]{:S(2)}) collective-permute-start(f32[3,16,128]{2,1,0:T(8,128)S(1)} %get-tuple-element.5), channel_id=1, source_target_pairs={{8,0},{16,8},{24,16},{32,24},{40,32},{48,40},{56,48},{64,56},{72,6... | collective-permute-start | bytes 73736 | tf_op jit(solution)/shard_map/ppermute | solution.py:178
  23.9 4.5 %collective-permute-start = (f32[3,16,128]{2,1,0:T(8,128)S(1)}, f32[3,16,128]{2,1,0:T(8,128)S(1)}, u32[]{:S(2)}, u32[]{:S(2)}) collective-permute-start(f32[3,16,128]{2,1,0:T(8,128)S(1)} %get-tuple-element.6), channel_id=1, source_target_pairs={{0,8},{8,16},{16,24},{24,32},{32,40},{40,48},{48,56},{56,64},{64,7... | collective-permute-start | bytes 73736 | tf_op jit(solution)/shard_map/ppermute | solution.py:177
  28.4 0.0 collective-permute-done.1.refs_5_
  28.4 1.5 %collective-permute-done.refs_3_ = f32[3,16,128]{2,1,0:T(8,128)S(1)} collective-permute-done((f32[3,16,128]{2,1,0:T(8,128)S(1)}, f32[3,16,128]{2,1,0:T(8,128)S(1)}, u32[]{:S(2)}, u32[]{:S(2)}) %collective-permute-start) | collective-permute-done | bytes 24608 | tf_op jit(solution)/shard_map/ppermute | solution.py:177
  29.9 0.0 copy-done.2
  29.9 0.0 copy-done.1
  29.9 0.0 copy-done.3
  29.9 1.9 %grads.1.grad_ref = f32[144,1024]{1,0:T(8,128)S(1)} custom-call(s32[6,1024]{1,0:T(8,128)S(1)} %copy-done.2, f32[3,6,1024]{2,1,0:T(8,128)S(1)} %copy-done.1, f32[1,1024]{1,0:T(1,128)S(1)} %bitcast.6, f32[3,16,128]{2,1,0:T(8,128)S(1)} %collective-permute-done.refs_3_, f32[3,16,1024]{2,1,0:T(8,128)S(1)} %copy-done, f32[3,16,128]{2,1,0:T(8,128)S(1)} %collective-permute-done.1.refs_5_), custom_call_target="tpu_custom_call" | custom-call | flops 8000000 | bytes 1000000 | tf_op jit(solution)/shard_map/grads/pallas_call | solution.py:68
  31.8 0.0 collective-permute-done.2.other_ref
  31.8 8.9 %tensor.1 = bf16[8,8,32,128]{3,2,1,0:T(8,128)(2,1)S(1)} custom-call(f32[144,1024]{1,0:T(8,128)S(1)} %grads.1.grad_ref, bf16[4,3,16,1024]{3,2,1,0:T(8,128)(2,1)S(1)} %all_to_all.15.own_ref, bf16[4,3,16,1024]{3,2,1,0:T(8,128)(2,1)S(1)} %collective-permute-done.2.other_ref), custom_call_target="tpu_custom_call" | custom-call | flops 1700000000 | bytes 2000000 | tf_op jit(solution)/shard_map/tensor/pallas_call | solution.py:132
  40.8 17.0 %all_to_all.16.tiles_ref = bf16[8,8,32,128]{3,2,1,0:T(8,128)(2,1)S(1)} all-to-all(bf16[8,8,32,128]{3,2,1,0:T(8,128)(2,1)S(1)} %tensor.1), channel_id=1, replica_groups=mesh['z'=8,'ylo'=2,'x'=4,'yhi'=4,'core'=2] {'ylo','x'}, dimensions={0} | all-to-all | bytes 1048576 | tf_op jit(solution)/shard_map/all_to_all | solution.py:183
  57.7 0.1 summed.2
  57.8 20.0 %all_to_all.17.tiles_ref = bf16[8,32,128]{2,1,0:T(8,128)(2,1)S(1)} all-to-all(bf16[8,32,128]{2,1,0:T(8,128)(2,1)S(1)} %summed.2), channel_id=1, replica_groups=mesh['z'=8,'ylo'=2,'x'=4,'yhi'=4,'core'=2] {'z'}, dimensions={0} | all-to-all | bytes 131072 | tf_op jit(solution)/shard_map/all_to_all | solution.py:185
  77.9 0.6 copy.7
  (3 shorter events, 0.1 us)
Async XLA Ops:
  1.0 21.6 %copy-start = (f32[3,16,1024]{2,1,0:T(8,128)S(1)}, f32[3,16,1024]{2,1,0:T(8,128)}, u32[]{:S(2)}) copy-start(f32[3,16,1024]{2,1,0:T(8,128)} %refs_4_.1) | copy-start | bytes 589828
  1.0 28.9 %copy-start.2 = (s32[6,1024]{1,0:T(8,128)S(1)}, s32[6,1024]{1,0:T(8,128)}, u32[]{:S(2)}) copy-start(s32[6,1024]{1,0:T(8,128)} %refs_0_.1) | copy-start | bytes 73732
  20.5 9.4 %copy-start.1 = (f32[3,6,1024]{2,1,0:T(8,128)S(1)}, f32[3,6,1024]{2,1,0:T(8,128)}, u32[]{:S(2)}) copy-start(f32[3,6,1024]{2,1,0:T(8,128)} %refs_1_.1) | copy-start | bytes 221188
  20.5 11.4 %collective-permute-start.2 = (bf16[4,3,16,1024]{3,2,1,0:T(8,128)(2,1)S(1)}, bf16[4,3,16,1024]{3,2,1,0:T(8,128)(2,1)S(1)}, u32[]{:S(2)}, u32[]{:S(2)}) collective-permute-start(bf16[4,3,16,1024]{3,2,1,0:T(8,128)(2,1)S(1)} %all_to_all.15.own_ref), channel_id=1, source_target_pairs={{0,1},{1,0},{2,3},{3,2},{4,5},{5,4},{6,7},{7,6},{8,9},{9,8},{10,11... | collective-permute-start | bytes 1179656 | tf_op jit(solution)/shard_map/ppermute | solution.py:180
  22.6 7.4 %copy-start.3 = (f32[1024]{0:T(1024)S(1)}, f32[1024]{0:T(1024)}, u32[]{:S(2)}) copy-start(f32[1024]{0:T(1024)} %param.6) | copy-start | bytes 12292
  22.6 5.9 %collective-permute-start.1 = (f32[3,16,128]{2,1,0:T(8,128)S(1)}, f32[3,16,128]{2,1,0:T(8,128)S(1)}, u32[]{:S(2)}, u32[]{:S(2)}) collective-permute-start(f32[3,16,128]{2,1,0:T(8,128)S(1)} %get-tuple-element.5), channel_id=1, source_target_pairs={{8,0},{16,8},{24,16},{32,24},{40,32},{48,40},{56,48},{64,56},{72,6... | collective-permute-start | bytes 73736 | tf_op jit(solution)/shard_map/ppermute | solution.py:178
  23.9 6.1 %collective-permute-start = (f32[3,16,128]{2,1,0:T(8,128)S(1)}, f32[3,16,128]{2,1,0:T(8,128)S(1)}, u32[]{:S(2)}, u32[]{:S(2)}) collective-permute-start(f32[3,16,128]{2,1,0:T(8,128)S(1)} %get-tuple-element.6), channel_id=1, source_target_pairs={{0,8},{8,16},{16,24},{24,32},{32,40},{40,48},{48,56},{56,64},{64,7... | collective-permute-start | bytes 73736 | tf_op jit(solution)/shard_map/ppermute | solution.py:177

commit v2 on v1

--- a/solution.py
+++ b/solution.py
@@ -11,8 +11,9 @@
 MODE = ("yhi", "core")
 PLANE = ("ylo", "x")
 GROUP = 4
+WIDE = 256
 LANES = 128
-TILE = 32
+TILE = 16
 
 
 def picked(block, lane):
@@ -76,93 +77,105 @@
     )(neighbours, stencil_coef, volumes.reshape(1, width), left, modes, right)
 
 
-def tensor_kernel(grad_ref, own_ref, other_ref, out_ref, wide_ref, flat_ref, held_a, held_b, rows_ref):
-    chips, comps, count, width = own_ref.shape
-    blocks = 2 * chips
-    total = blocks * count
-    core = lax.axis_index("core")
+def tensor_kernel(flat_order, *refs):
+    grad_ref, lows = refs[0], refs[1:-6]
+    out_ref, wide_ref, flat_ref, held_a, held_b, rows_ref = refs[-6:]
+    chips, comps, count, width = lows[0].shape
+    total = sum(ref.shape[0] for ref in lows) * count
+    core = 0 if flat_order else lax.axis_index("core")
     for c in range(comps):
-        for h, ref in ((0, own_ref), (1, other_ref)):
-            place = core if h == 0 else 1 - core
+        for h, ref in enumerate(lows):
             for y in range(chips):
-                row = pl.multiple_of((2 * y + place) * count, count)
+                if flat_order:
+                    row = y * count
+                else:
+                    row = pl.multiple_of((2 * y + (core if h == 0 else 1 - core)) * count, count)
                 piece = ref[y, c]
                 flat_ref[pl.ds(row, count), pl.ds(c * width, width)] = piece
                 wide_ref[c, pl.ds(row, count), :] = piece.astype(jnp.float32)
 
-    def build(group, held):
-        for x in range(0, width, LANES):
-            at = slice(x, x + LANES)
-            for j in range(0, total, TILE):
-                low = [wide_ref[d, j : j + TILE, at] for d in range(3)]
-                for kk in range(GROUP):
-                    k = group * GROUP + kk
-                    for c in range(comps):
-                        row = [grad_ref[pl.ds((d * comps + c) * count + k, 1), at] for d in range(3)]
-                        mixed = low[0] * row[0] + low[1] * row[1] + low[2] * row[2]
-                        held[kk * total + j : kk * total + j + TILE, c * width + x : c * width + x + LANES] = (
-                            mixed.astype(jnp.bfloat16)
-                        )
-
-    def contract(group, held):
-        part = lax.dot_general(
-            held[...], flat_ref[...], (((1,), (1,)), ((), ())), preferred_element_type=jnp.float32
+    def build(group, x, c, held):
+        at = slice(x, x + WIDE)
+        for j in range(0, total, TILE):
+            low = [wide_ref[d, j : j + TILE, at] for d in range(3)]
+            for kk in range(GROUP):
+                k = group * GROUP + kk
+                row = [grad_ref[pl.ds((d * comps + c) * count + k, 1), at] for d in range(3)]
+                mixed = low[0] * row[0] + low[1] * row[1] + low[2] * row[2]
+                held[kk * total + j : kk * total + j + TILE, :] = mixed.astype(jnp.bfloat16)
+
+    def contract(x, c, held, part):
+        more = lax.dot_general(
+            held[...],
+            flat_ref[:, c * width + x : c * width + x + WIDE],
+            (((1,), (1,)), ((), ())),
+            preferred_element_type=jnp.float32,
         )
+        return more if part is None else part + more
+
+    def finish(group, part):
         for kk in range(GROUP):
             k = group * GROUP + kk
             rows_ref[pl.ds(k, total, stride=count), :] = part[kk * total : (kk + 1) * total].T
 
-    groups = count // GROUP
     helds = (held_a, held_b)
-    build(0, helds[0])
-    for g in range(groups):
-        if g + 1 < groups:
-            build(g + 1, helds[(g + 1) % 2])
-        contract(g, helds[g % 2])
+    work = [(g, x, c) for g in range(count // GROUP) for x in range(0, width, WIDE) for c in range(comps)]
+    each = len(work) // (count // GROUP)
+    build(*work[0], helds[0])
+    part = None
+    for n, (g, x, c) in enumerate(work):
+        if n + 1 < len(work):
+            build(*work[n + 1], helds[(n + 1) % 2])
+        part = contract(x, c, helds[n % 2], part)
+        if n % each == each - 1:
+            finish(g, part)
+            part = None
     first, second, size = out_ref.shape[:3]
     for a in range(first):
         for b in range(second):
-            out_ref[a, b] = rows_ref[pl.ds((b * first + a) * size, size), :].astype(jnp.bfloat16)
-
-
-def local_tensor(grads, own, other, plane, depth):
-    chips, comps, count, width = own.shape
-    total = 2 * chips * count
+            out_ref[a, b] = rows_ref[pl.ds((a * second + b) * size, size), :].astype(jnp.bfloat16)
+
+
+def local_tensor(grads, lows, plane, depth):
+    comps, count, width = lows[0].shape[1:]
+    total = sum(low.shape[0] for low in lows) * count
     rows = 2 * count
     return pl.pallas_call(
-        tensor_kernel,
+        lambda *refs: tensor_kernel(len(lows) == 1, *refs),
         out_shape=jax.ShapeDtypeStruct((plane, depth, rows, total), jnp.bfloat16),
-        in_specs=[pl.BlockSpec(memory_space=pltpu.VMEM)] * 3,
+        in_specs=[pl.BlockSpec(memory_space=pltpu.VMEM)] * (1 + len(lows)),
         out_specs=pl.BlockSpec(memory_space=pltpu.VMEM),
         scratch_shapes=[
             pltpu.VMEM((comps, total, width), jnp.float32),
             pltpu.VMEM((total, comps * width), jnp.bfloat16),
-            pltpu.VMEM((GROUP * total, comps * width), jnp.bfloat16),
-            pltpu.VMEM((GROUP * total, comps * width), jnp.bfloat16),
+            pltpu.VMEM((GROUP * total, WIDE), jnp.bfloat16),
+            pltpu.VMEM((GROUP * total, WIDE), jnp.bfloat16),
             pltpu.VMEM((count * total, total), jnp.float32),
         ],
         compiler_params=pltpu.CompilerParams(vmem_limit_bytes=16 << 20),
         cost_estimate=pl.CostEstimate(flops=1_700_000_000, bytes_accessed=2_000_000, transcendentals=0),
         name="tensor",
-    )(grads, own, other)
-
-
-def sum_kernel(tiles_ref, out_ref):
+    )(grads, *lows)
+
+
+def placed_kernel(tiles_ref, out_ref):
     total = tiles_ref[0].astype(jnp.float32)
     for i in range(1, tiles_ref.shape[0]):
         total = total + tiles_ref[i].astype(jnp.float32)
-    out_ref[...] = total.astype(out_ref.dtype)
-
-
-def summed(tiles, dtype):
+    count, pairs = out_ref.shape[:2]
+    for i in range(pairs):
+        out_ref[:, i, :] = total[i * count : (i + 1) * count]
+
+
+def placed(tiles, count):
+    rows, total = tiles.shape[1:]
     return pl.pallas_call(
-        sum_kernel,
-        out_shape=jax.ShapeDtypeStruct(tiles.shape[1:], dtype),
+        placed_kernel,
+        out_shape=jax.ShapeDtypeStruct((count, rows // count, total), jnp.float32),
         in_specs=[pl.BlockSpec(memory_space=pltpu.VMEM)],
         out_specs=pl.BlockSpec(memory_space=pltpu.VMEM),
         compiler_params=pltpu.CompilerParams(vmem_limit_bytes=4 << 20),
-        cost_estimate=pl.CostEstimate(flops=300_000, bytes_accessed=600_000, transcendentals=0),
-        name="summed",
+        name="placed",
     )(tiles)
 
 
@@ -177,14 +190,13 @@
     left = lax.ppermute(modes[:, :, width - LANES :], SPACE, [(i, i + 1) for i in range(last)])
     right = lax.ppermute(modes[:, :, :LANES], SPACE, [(i + 1, i) for i in range(last)])
     grads = weighted_grads(modes, left, right, stencil_coef, volumes, neighbours, 1.0 / math.sqrt(cells))
+    own, grads = lax.optimization_barrier((own, grads))
     other = lax.ppermute(own, "core", [(0, 1), (1, 0)])
+    lows = (own, other)
     plane, depth = lax.axis_size(PLANE), lax.axis_size("z")
-    share = local_tensor(grads, own, other, plane, depth)
-    first = lax.all_to_all(share, PLANE, 0, 0, tiled=True)
-    partial = summed(first, jnp.bfloat16)
-    second = lax.all_to_all(partial, "z", 0, 0, tiled=True)
-    rows = summed(second, jnp.float32)
-    return jnp.transpose(rows.reshape(2, count, -1), (1, 0, 2))
+    share = local_tensor(grads, lows, plane, depth)
+    second = lax.all_to_all(share.reshape(plane * depth, 2 * count, -1), SPACE, 0, 0, tiled=True)
+    return placed(second, count)
 
 
 def solution(mesh):

time: 78.8 us -> 66.2 us (0.84)
  blocking collectives: 56.5 us -> 35 us
  starting transfers between devices: 7.88 us -> 17.1 us
  Pallas kernels: 10.9 us -> 8.34 us
  waiting for transfers between devices: 1.5 us -> 3.68 us
    all_to_all x3 -> x1, blocking collectives: 56.5 us -> 35 us  [body(): lax.all_to_all(share.reshape(plane * depth, 2 * count, -1), SPACE, 0, 0,...]
    all_to_all x0 -> x1, starting transfers between devices: none -> 9.24 us  [body(): own = lax.all_to_all(copies, 'yhi', 0, 0, tiled=True)]
    pallas_call x3 -> x2, Pallas kernels: 8.99 us -> 6.45 us  [the longest x1 5.73 us: local_tensor(): pl.pallas_call(lambda *refs: tensor_kernel(len(lows) == 1, *refs), out_sh...]
    ppermute x1, waiting for transfers between devices: 0.01 us -> 1.69 us  [body(): other = lax.ppermute(own, 'core', [(0, 1), (1, 0)])]
  transfers between devices with their start and end apart: 3 -> 4, of which waited for: 1 -> 3; matrix products, arithmetic and copies ran while one was open for 0% -> 0% of each run, Pallas kernels for 2% -> 3%
where the time goes in v2:
time: 66.2 us; the launch traced here: 65.9 us
  blocking collectives  35 us (53%)
  starting transfers between devices  17.1 us (26%)
  Pallas kernels  8.34 us (13%)
  waiting for transfers between devices  3.68 us (6%)
  other arithmetic  0.94 us (1%)
  local copies, waits for them, and re-layouts  0.8 us (1%)
    all_to_all x1, blocking collectives, body(): lax.all_to_all(share.reshape(plane * depth, 2 * count, -1), SPACE, 0, 0,...  35 us
    all_to_all x1, starting transfers between devices, body(): own = lax.all_to_all(copies, 'yhi', 0, 0, tiled=True)  9.24 us
    pallas_call x1, Pallas kernels, local_tensor(): pl.pallas_call(lambda *refs: tensor_kernel(len(lows) == 1, *refs), out_sh...  5.73 us
    ppermute x1, starting transfers between devices, body(): lax.ppermute(modes[:, :, width - LANES:], SPACE, [(i, i + 1) for i in ran...  4.55 us
    ppermute x1, starting transfers between devices, body(): other = lax.ppermute(own, 'core', [(0, 1), (1, 0)])  1.91 us
    pallas_call x1, Pallas kernels, weighted_grads(): pl.pallas_call(lambda *refs: grads_kernel(scale, *refs), out_shape=jax.Sh...  1.89 us
    ppermute x1, waiting for transfers between devices, body(): other = lax.ppermute(own, 'core', [(0, 1), (1, 0)])  1.69 us
    ppermute x1, waiting for transfers between devices, body(): lax.ppermute(modes[:, :, width - LANES:], SPACE, [(i, i + 1) for i in ran...  1.49 us
  transfers between devices with their start and end apart: 4, of which 3 were waited for; matrix products, arithmetic and copies ran while one was open for 0% of the time, Pallas kernels for 3%

profile of v2, /device:TPU:16, one launch (start us, length us, event | category | flops | bytes accessed | tf_op | source)
XLA Modules:
  0.0 65.9 jit_solution(8652645208838908240)
XLA Ops:
  0.0 0.9 %convert_element_type.3 = bf16[3,16,1024]{2,1,0:T(8,128)(2,1)S(1)} convert(f32[3,16,1024]{2,1,0:T(8,128)} %refs_4_.1) | non-fusion elementwise | flops 49152 | bytes 294912 | tf_op jit(solution)/shard_map/convert_element_type | solution.py:185
  0.9 0.8 %broadcast_in_dim.3 = bf16[4,3,16,1024]{3,2,1,0:T(8,128)(2,1)} broadcast(bf16[3,16,1024]{2,1,0:T(8,128)(2,1)S(1)} %convert_element_type.3), dimensions={1,2,3} | broadcast | bytes 491520 | tf_op jit(solution)/shard_map/broadcast_in_dim | solution.py:187
  1.7 0.0 copy-start
  1.7 0.0 copy-start.2
  1.7 9.2 %all-to-all-start = ((bf16[4,3,16,1024]{3,2,1,0:T(8,128)(2,1)}), bf16[4,3,16,1024]{3,2,1,0:T(8,128)(2,1)S(1)}, u32[]{:S(2)}, u32[]{:S(2)}) async-start(bf16[4,3,16,1024]{3,2,1,0:T(8,128)(2,1)} %broadcast_in_dim.3), calls=%async_computation | async-start | bytes 786432 | tf_op jit(solution)/shard_map/all_to_all | solution.py:188
  11.0 0.0 copy-done
  11.0 0.0 copy-start.1
  11.0 0.0 copy-start.3
  11.0 1.4 %collective-permute-start.1 = (f32[3,16,128]{2,1,0:T(8,128)S(1)}, f32[3,16,128]{2,1,0:T(8,128)S(1)}, u32[]{:S(2)}, u32[]{:S(2)}) collective-permute-start(f32[3,16,128]{2,1,0:T(8,128)S(1)} %get-tuple-element.9), channel_id=1, source_target_pairs={{8,0},{16,8},{24,16},{32,24},{40,32},{48,40},{56,48},{64,56},{72,6... | collective-permute-start | bytes 73736 | tf_op jit(solution)/shard_map/ppermute | solution.py:191
  12.4 4.5 %collective-permute-start = (f32[3,16,128]{2,1,0:T(8,128)S(1)}, f32[3,16,128]{2,1,0:T(8,128)S(1)}, u32[]{:S(2)}, u32[]{:S(2)}) collective-permute-start(f32[3,16,128]{2,1,0:T(8,128)S(1)} %get-tuple-element.10), channel_id=1, source_target_pairs={{0,8},{8,16},{16,24},{24,32},{32,40},{40,48},{48,56},{56,64},{64,7... | collective-permute-start | bytes 73736 | tf_op jit(solution)/shard_map/ppermute | solution.py:190
  17.0 0.0 collective-permute-done.1.refs_5_
  17.0 1.5 %collective-permute-done.refs_3_ = f32[3,16,128]{2,1,0:T(8,128)S(1)} collective-permute-done((f32[3,16,128]{2,1,0:T(8,128)S(1)}, f32[3,16,128]{2,1,0:T(8,128)S(1)}, u32[]{:S(2)}, u32[]{:S(2)}) %collective-permute-start) | collective-permute-done | bytes 24608 | tf_op jit(solution)/shard_map/ppermute | solution.py:190
  18.5 0.0 copy-done.2
  18.5 0.0 copy-done.1
  18.5 0.0 copy-done.3
  18.5 1.9 %grads.1.refs_0_ = f32[144,1024]{1,0:T(8,128)S(1)} custom-call(s32[6,1024]{1,0:T(8,128)S(1)} %copy-done.2, f32[3,6,1024]{2,1,0:T(8,128)S(1)} %copy-done.1, f32[1,1024]{1,0:T(1,128)S(1)} %bitcast.3, f32[3,16,128]{2,1,0:T(8,128)S(1)} %collective-permute-done.refs_3_, f32[3,16,1024]{2,1,0:T(8,128)S(1)} %copy-done, f32[3,16,128]{2,1,0:T(8,128)S(1)} %collective-permute-done.1.refs_5_), custom_call_target="tpu_custom_call" | custom-call | flops 8000000 | bytes 1000000 | tf_op jit(solution)/shard_map/grads/pallas_call | solution.py:69
  20.4 0.5 all-to-all-done.refs_1_
  20.9 1.9 %collective-permute-start.2 = (bf16[4,3,16,1024]{3,2,1,0:T(8,128)(2,1)S(1)}, bf16[4,3,16,1024]{3,2,1,0:T(8,128)(2,1)S(1)}, u32[]{:S(2)}, u32[]{:S(2)}) collective-permute-start(bf16[4,3,16,1024]{3,2,1,0:T(8,128)(2,1)S(1)} %all-to-all-done.refs_1_), channel_id=1, source_target_pairs={{0,1},{1,0},{2,3},{3,2},{4,5},{5,4},{6,7},{7,6},{8,9},{9,8},{10,11... | collective-permute-start | bytes 1179656 | tf_op jit(solution)/shard_map/ppermute | solution.py:194
  22.8 1.7 %collective-permute-done.2.refs_2_ = bf16[4,3,16,1024]{3,2,1,0:T(8,128)(2,1)S(1)} collective-permute-done((bf16[4,3,16,1024]{3,2,1,0:T(8,128)(2,1)S(1)}, bf16[4,3,16,1024]{3,2,1,0:T(8,128)(2,1)S(1)}, u32[]{:S(2)}, u32[]{:S(2)}) %collective-permute-start.2) | collective-permute-done | bytes 393248 | tf_op jit(solution)/shard_map/ppermute | solution.py:194
  24.5 5.7 %tensor.1 = bf16[8,8,32,128]{3,2,1,0:T(8,128)(2,1)S(1)} custom-call(f32[144,1024]{1,0:T(8,128)S(1)} %grads.1.refs_0_, bf16[4,3,16,1024]{3,2,1,0:T(8,128)(2,1)S(1)} %all-to-all-done.refs_1_, bf16[4,3,16,1024]{3,2,1,0:T(8,128)(2,1)S(1)} %collective-permute-done.2.refs_2_), custom_call_target="tpu_custom_call" | custom-call | flops 1700000000 | bytes 2000000 | tf_op jit(solution)/shard_map/tensor/pallas_call | solution.py:143
  30.2 35.0 %all_to_all.10.tiles_ref = bf16[64,32,128]{2,1,0:T(8,128)(2,1)S(1)} all-to-all(bf16[64,32,128]{2,1,0:T(8,128)(2,1)S(1)} %bitcast.2), channel_id=1, replica_groups=mesh['z'=8,'ylo'=2,'x'=4,'yhi'=4,'core'=2] {'z','ylo','x'}, dimensions={0} | all-to-all | bytes 1048576 | tf_op jit(solution)/shard_map/all_to_all | solution.py:198
  65.2 0.7 %placed.1 = f32[16,2,128]{2,1,0:T(2,128)} custom-call(bf16[64,32,128]{2,1,0:T(8,128)(2,1)S(1)} %all_to_all.10.tiles_ref), custom_call_target="tpu_custom_call" | custom-call | tf_op jit(solution)/shard_map/placed/pallas_call | solution.py:172
  (1 shorter events, 0.0 us)
Async XLA Ops:
  1.7 9.2 %copy-start = (f32[3,16,1024]{2,1,0:T(8,128)S(1)}, f32[3,16,1024]{2,1,0:T(8,128)}, u32[]{:S(2)}) copy-start(f32[3,16,1024]{2,1,0:T(8,128)} %refs_4_.1) | copy-start | bytes 589828
  1.7 16.8 %copy-start.2 = (s32[6,1024]{1,0:T(8,128)S(1)}, s32[6,1024]{1,0:T(8,128)}, u32[]{:S(2)}) copy-start(s32[6,1024]{1,0:T(8,128)} %refs_0_.1) | copy-start | bytes 73732
  1.7 19.2 %all-to-all-start = ((bf16[4,3,16,1024]{3,2,1,0:T(8,128)(2,1)}), bf16[4,3,16,1024]{3,2,1,0:T(8,128)(2,1)S(1)}, u32[]{:S(2)}, u32[]{:S(2)}) async-start(bf16[4,3,16,1024]{3,2,1,0:T(8,128)(2,1)} %broadcast_in_dim.3), calls=%async_computation | async-start | bytes 786432 | tf_op jit(solution)/shard_map/all_to_all | solution.py:188
  11.0 7.5 %copy-start.1 = (f32[3,6,1024]{2,1,0:T(8,128)S(1)}, f32[3,6,1024]{2,1,0:T(8,128)}, u32[]{:S(2)}) copy-start(f32[3,6,1024]{2,1,0:T(8,128)} %refs_1_.1) | copy-start | bytes 221188
  11.0 7.5 %copy-start.3 = (f32[1024]{0:T(1024)S(1)}, f32[1024]{0:T(1024)}, u32[]{:S(2)}) copy-start(f32[1024]{0:T(1024)} %param.6) | copy-start | bytes 12292
  11.0 6.0 %collective-permute-start.1 = (f32[3,16,128]{2,1,0:T(8,128)S(1)}, f32[3,16,128]{2,1,0:T(8,128)S(1)}, u32[]{:S(2)}, u32[]{:S(2)}) collective-permute-start(f32[3,16,128]{2,1,0:T(8,128)S(1)} %get-tuple-element.9), channel_id=1, source_target_pairs={{8,0},{16,8},{24,16},{32,24},{40,32},{48,40},{56,48},{64,56},{72,6... | collective-permute-start | bytes 73736 | tf_op jit(solution)/shard_map/ppermute | solution.py:191
  12.4 6.1 %collective-permute-start = (f32[3,16,128]{2,1,0:T(8,128)S(1)}, f32[3,16,128]{2,1,0:T(8,128)S(1)}, u32[]{:S(2)}, u32[]{:S(2)}) collective-permute-start(f32[3,16,128]{2,1,0:T(8,128)S(1)} %get-tuple-element.10), channel_id=1, source_target_pairs={{0,8},{8,16},{16,24},{24,32},{32,40},{40,48},{48,56},{56,64},{64,7... | collective-permute-start | bytes 73736 | tf_op jit(solution)/shard_map/ppermute | solution.py:190
  20.9 3.6 %collective-permute-start.2 = (bf16[4,3,16,1024]{3,2,1,0:T(8,128)(2,1)S(1)}, bf16[4,3,16,1024]{3,2,1,0:T(8,128)(2,1)S(1)}, u32[]{:S(2)}, u32[]{:S(2)}) collective-permute-start(bf16[4,3,16,1024]{3,2,1,0:T(8,128)(2,1)S(1)} %all-to-all-done.refs_1_), channel_id=1, source_target_pairs={{0,1},{1,0},{2,3},{3,2},{4,5},{5,4},{6,7},{7,6},{8,9},{9,8},{10,11... | collective-permute-start | bytes 1179656 | tf_op jit(solution)/shard_map/ppermute | solution.py:194

commit v3 on v2

--- a/solution.py
+++ b/solution.py
@@ -9,7 +9,6 @@
 
 SPACE = ("z", "ylo", "x")
 MODE = ("yhi", "core")
-PLANE = ("ylo", "x")
 GROUP = 4
 WIDE = 256
 LANES = 128
@@ -77,24 +76,23 @@
     )(neighbours, stencil_coef, volumes.reshape(1, width), left, modes, right)
 
 
-def tensor_kernel(flat_order, *refs):
-    grad_ref, lows = refs[0], refs[1:-6]
-    out_ref, wide_ref, flat_ref, held_a, held_b, rows_ref = refs[-6:]
-    chips, comps, count, width = lows[0].shape
-    total = sum(ref.shape[0] for ref in lows) * count
-    core = 0 if flat_order else lax.axis_index("core")
-    for c in range(comps):
-        for h, ref in enumerate(lows):
-            for y in range(chips):
-                if flat_order:
-                    row = y * count
-                else:
-                    row = pl.multiple_of((2 * y + (core if h == 0 else 1 - core)) * count, count)
-                piece = ref[y, c]
-                flat_ref[pl.ds(row, count), pl.ds(c * width, width)] = piece
-                wide_ref[c, pl.ds(row, count), :] = piece.astype(jnp.float32)
+def tensor_kernel(absolute, grad_ref, own_ref, other_ref, out_ref, wide_ref, flat_ref, held_a, held_b, rows_ref):
+    chips, comps, count, width = own_ref.shape
+    blocks = 2 * chips
+    total = blocks * count
+
+    def spread(x):
+        for y in range(chips):
+            for h, ref in enumerate((own_ref, other_ref)):
+                rows = slice((2 * y + h) * count, (2 * y + h + 1) * count)
+                for c in range(comps):
+                    piece = ref[y, c, :, x : x + WIDE]
+                    flat_ref[rows, c * width + x : c * width + x + WIDE] = piece
+                    wide_ref[c, rows, x : x + WIDE] = piece.astype(jnp.float32)
 
     def build(group, x, c, held):
+        if group == 0 and c == 0:
+            spread(x)
         at = slice(x, x + WIDE)
         for j in range(0, total, TILE):
             low = [wide_ref[d, j : j + TILE, at] for d in range(3)]
@@ -130,20 +128,20 @@
         if n % each == each - 1:
             finish(g, part)
             part = None
-    first, second, size = out_ref.shape[:3]
-    for a in range(first):
-        for b in range(second):
-            out_ref[a, b] = rows_ref[pl.ds((a * second + b) * size, size), :].astype(jnp.bfloat16)
-
-
-def local_tensor(grads, lows, plane, depth):
-    comps, count, width = lows[0].shape[1:]
-    total = sum(low.shape[0] for low in lows) * count
-    rows = 2 * count
+    size = out_ref.shape[1]
+    each = out_ref.shape[0] // blocks
+    for r in range(blocks):
+        rows = rows_ref[r * each * size : (r + 1) * each * size, :].astype(jnp.bfloat16)
+        out_ref[pl.ds(absolute(r) * each, each)] = rows.reshape(each, size, total)
+
+
+def local_tensor(grads, own, other, shards, absolute):
+    chips, comps, count, width = own.shape
+    total = 2 * chips * count
     return pl.pallas_call(
-        lambda *refs: tensor_kernel(len(lows) == 1, *refs),
-        out_shape=jax.ShapeDtypeStruct((plane, depth, rows, total), jnp.bfloat16),
-        in_specs=[pl.BlockSpec(memory_space=pltpu.VMEM)] * (1 + len(lows)),
+        lambda *refs: tensor_kernel(absolute, *refs),
+        out_shape=jax.ShapeDtypeStruct((shards, total * count // shards, total), jnp.bfloat16),
+        in_specs=[pl.BlockSpec(memory_space=pltpu.VMEM)] * 3,
         out_specs=pl.BlockSpec(memory_space=pltpu.VMEM),
         scratch_shapes=[
             pltpu.VMEM((comps, total, width), jnp.float32),
@@ -155,22 +153,25 @@
         compiler_params=pltpu.CompilerParams(vmem_limit_bytes=16 << 20),
         cost_estimate=pl.CostEstimate(flops=1_700_000_000, bytes_accessed=2_000_000, transcendentals=0),
         name="tensor",
-    )(grads, *lows)
-
-
-def placed_kernel(tiles_ref, out_ref):
+    )(grads, own, other)
+
+
+def placed_kernel(relative, tiles_ref, out_ref):
     total = tiles_ref[0].astype(jnp.float32)
     for i in range(1, tiles_ref.shape[0]):
         total = total + tiles_ref[i].astype(jnp.float32)
-    count, pairs = out_ref.shape[:2]
+    count, pairs, modes = out_ref.shape
+    place = lax.broadcasted_iota(jnp.int32, (8, modes), 1)
+    lane = relative(place >> 4) * 16 + (place & 15)
     for i in range(pairs):
-        out_ref[:, i, :] = total[i * count : (i + 1) * count]
-
-
-def placed(tiles, count):
+        for r in range(0, count, 8):
+            out_ref[r : r + 8, i, :] = picked(total[i * count + r : i * count + r + 8], lane)
+
+
+def placed(tiles, count, relative):
     rows, total = tiles.shape[1:]
     return pl.pallas_call(
-        placed_kernel,
+        lambda *refs: placed_kernel(relative, *refs),
         out_shape=jax.ShapeDtypeStruct((count, rows // count, total), jnp.float32),
         in_specs=[pl.BlockSpec(memory_space=pltpu.VMEM)],
         out_specs=pl.BlockSpec(memory_space=pltpu.VMEM),
@@ -192,11 +193,13 @@
     grads = weighted_grads(modes, left, right, stencil_coef, volumes, neighbours, 1.0 / math.sqrt(cells))
     own, grads = lax.optimization_barrier((own, grads))
     other = lax.ppermute(own, "core", [(0, 1), (1, 0)])
-    lows = (own, other)
-    plane, depth = lax.axis_size(PLANE), lax.axis_size("z")
-    share = local_tensor(grads, lows, plane, depth)
-    second = lax.all_to_all(share.reshape(plane * depth, 2 * count, -1), SPACE, 0, 0, tiled=True)
-    return placed(second, count)
+    def swapped(block):
+        return block ^ lax.axis_index("core")
+
+    absolute, relative = swapped, swapped
+    share = local_tensor(grads, own, other, lax.axis_size(SPACE), absolute)
+    tiles = lax.all_to_all(share, SPACE, 0, 0, tiled=True)
+    return placed(tiles, count, relative)
 
 
 def solution(mesh):

time: 66.2 us -> 65.4 us (0.988)
  Pallas kernels: 8.34 us -> 7.59 us
    pallas_call x2, Pallas kernels: 6.45 us -> 5.7 us  [the longest x1 4.92 us: local_tensor(): pl.pallas_call(lambda *refs: tensor_kernel(absolute, *refs), out_shape=ja...]
where the time goes in v3:
time: 65.4 us; the launch traced here: 65.1 us
  blocking collectives  34.9 us (53%)
  starting transfers between devices  17.1 us (26%)
  Pallas kernels  7.59 us (12%)
  waiting for transfers between devices  3.68 us (6%)
  other arithmetic  0.94 us (1%)
  local copies, waits for them, and re-layouts  0.8 us (1%)
    all_to_all x1, blocking collectives, body(): tiles = lax.all_to_all(share, SPACE, 0, 0, tiled=True)  34.9 us
    all_to_all x1, starting transfers between devices, body(): own = lax.all_to_all(copies, 'yhi', 0, 0, tiled=True)  9.24 us
    pallas_call x1, Pallas kernels, local_tensor(): pl.pallas_call(lambda *refs: tensor_kernel(absolute, *refs), out_shape=ja...  4.92 us
    ppermute x1, starting transfers between devices, body(): lax.ppermute(modes[:, :, width - LANES:], SPACE, [(i, i + 1) for i in ran...  4.55 us
    ppermute x1, starting transfers between devices, body(): other = lax.ppermute(own, 'core', [(0, 1), (1, 0)])  1.91 us
    pallas_call x1, Pallas kernels, weighted_grads(): pl.pallas_call(lambda *refs: grads_kernel(scale, *refs), out_shape=jax.Sh...  1.89 us
    ppermute x1, waiting for transfers between devices, body(): other = lax.ppermute(own, 'core', [(0, 1), (1, 0)])  1.69 us
    ppermute x1, waiting for transfers between devices, body(): lax.ppermute(modes[:, :, width - LANES:], SPACE, [(i, i + 1) for i in ran...  1.49 us
  transfers between devices with their start and end apart: 4, of which 3 were waited for; matrix products, arithmetic and copies ran while one was open for 0% of the time, Pallas kernels for 3%

profile of v3, /device:TPU:16, one launch (start us, length us, event | category | flops | bytes accessed | tf_op | source)
XLA Modules:
  0.0 65.1 jit_solution(14896683060899816475)
XLA Ops:
  0.0 0.9 %convert_element_type.3 = bf16[3,16,1024]{2,1,0:T(8,128)(2,1)S(1)} convert(f32[3,16,1024]{2,1,0:T(8,128)} %refs_4_.1) | non-fusion elementwise | flops 49152 | bytes 294912 | tf_op jit(solution)/shard_map/convert_element_type | solution.py:186
  0.9 0.8 %broadcast_in_dim.3 = bf16[4,3,16,1024]{3,2,1,0:T(8,128)(2,1)} broadcast(bf16[3,16,1024]{2,1,0:T(8,128)(2,1)S(1)} %convert_element_type.3), dimensions={1,2,3} | broadcast | bytes 491520 | tf_op jit(solution)/shard_map/broadcast_in_dim | solution.py:188
  1.7 0.0 copy-start
  1.7 0.0 copy-start.2
  1.7 9.2 %all-to-all-start = ((bf16[4,3,16,1024]{3,2,1,0:T(8,128)(2,1)}), bf16[4,3,16,1024]{3,2,1,0:T(8,128)(2,1)S(1)}, u32[]{:S(2)}, u32[]{:S(2)}) async-start(bf16[4,3,16,1024]{3,2,1,0:T(8,128)(2,1)} %broadcast_in_dim.3), calls=%async_computation | async-start | bytes 786432 | tf_op jit(solution)/shard_map/all_to_all | solution.py:189
  11.0 0.0 copy-done
  11.0 0.0 copy-start.1
  11.0 0.0 copy-start.3
  11.0 1.4 %collective-permute-start.1 = (f32[3,16,128]{2,1,0:T(8,128)S(1)}, f32[3,16,128]{2,1,0:T(8,128)S(1)}, u32[]{:S(2)}, u32[]{:S(2)}) collective-permute-start(f32[3,16,128]{2,1,0:T(8,128)S(1)} %get-tuple-element.9), channel_id=1, source_target_pairs={{8,0},{16,8},{24,16},{32,24},{40,32},{48,40},{56,48},{64,56},{72,6... | collective-permute-start | bytes 73736 | tf_op jit(solution)/shard_map/ppermute | solution.py:192
  12.4 4.5 %collective-permute-start = (f32[3,16,128]{2,1,0:T(8,128)S(1)}, f32[3,16,128]{2,1,0:T(8,128)S(1)}, u32[]{:S(2)}, u32[]{:S(2)}) collective-permute-start(f32[3,16,128]{2,1,0:T(8,128)S(1)} %get-tuple-element.10), channel_id=1, source_target_pairs={{0,8},{8,16},{16,24},{24,32},{32,40},{40,48},{48,56},{56,64},{64,7... | collective-permute-start | bytes 73736 | tf_op jit(solution)/shard_map/ppermute | solution.py:191
  17.0 0.0 collective-permute-done.1.refs_5_
  17.0 1.5 %collective-permute-done.refs_3_ = f32[3,16,128]{2,1,0:T(8,128)S(1)} collective-permute-done((f32[3,16,128]{2,1,0:T(8,128)S(1)}, f32[3,16,128]{2,1,0:T(8,128)S(1)}, u32[]{:S(2)}, u32[]{:S(2)}) %collective-permute-start) | collective-permute-done | bytes 24608 | tf_op jit(solution)/shard_map/ppermute | solution.py:191
  18.5 0.0 copy-done.2
  18.5 0.0 copy-done.1
  18.5 0.0 copy-done.3
  18.5 1.9 %grads.1.refs_0_ = f32[144,1024]{1,0:T(8,128)S(1)} custom-call(s32[6,1024]{1,0:T(8,128)S(1)} %copy-done.2, f32[3,6,1024]{2,1,0:T(8,128)S(1)} %copy-done.1, f32[1,1024]{1,0:T(1,128)S(1)} %bitcast.1, f32[3,16,128]{2,1,0:T(8,128)S(1)} %collective-permute-done.refs_3_, f32[3,16,1024]{2,1,0:T(8,128)S(1)} %copy-done, f32[3,16,128]{2,1,0:T(8,128)S(1)} %collective-permute-done.1.refs_5_), custom_call_target="tpu_custom_call" | custom-call | flops 8000000 | bytes 1000000 | tf_op jit(solution)/shard_map/grads/pallas_call | solution.py:68
  20.4 0.5 all-to-all-done.refs_1_
  20.9 1.9 %collective-permute-start.2 = (bf16[4,3,16,1024]{3,2,1,0:T(8,128)(2,1)S(1)}, bf16[4,3,16,1024]{3,2,1,0:T(8,128)(2,1)S(1)}, u32[]{:S(2)}, u32[]{:S(2)}) collective-permute-start(bf16[4,3,16,1024]{3,2,1,0:T(8,128)(2,1)S(1)} %all-to-all-done.refs_1_), channel_id=1, source_target_pairs={{0,1},{1,0},{2,3},{3,2},{4,5},{5,4},{6,7},{7,6},{8,9},{9,8},{10,11... | collective-permute-start | bytes 1179656 | tf_op jit(solution)/shard_map/ppermute | solution.py:195
  22.8 1.7 %collective-permute-done.2.refs_2_ = bf16[4,3,16,1024]{3,2,1,0:T(8,128)(2,1)S(1)} collective-permute-done((bf16[4,3,16,1024]{3,2,1,0:T(8,128)(2,1)S(1)}, bf16[4,3,16,1024]{3,2,1,0:T(8,128)(2,1)S(1)}, u32[]{:S(2)}, u32[]{:S(2)}) %collective-permute-start.2) | collective-permute-done | bytes 393248 | tf_op jit(solution)/shard_map/ppermute | solution.py:195
  24.5 4.9 %tensor.1 = bf16[64,32,128]{2,1,0:T(8,128)(2,1)S(1)} custom-call(f32[144,1024]{1,0:T(8,128)S(1)} %grads.1.refs_0_, bf16[4,3,16,1024]{3,2,1,0:T(8,128)(2,1)S(1)} %all-to-all-done.refs_1_, bf16[4,3,16,1024]{3,2,1,0:T(8,128)(2,1)S(1)} %collective-permute-done.2.refs_2_), custom_call_target="tpu_custom_call" | custom-call | flops 1700000000 | bytes 2000000 | tf_op jit(solution)/shard_map/tensor/pallas_call | solution.py:141
  29.4 34.9 %all_to_all.10.refs_0_ = bf16[64,32,128]{2,1,0:T(8,128)(2,1)S(1)} all-to-all(bf16[64,32,128]{2,1,0:T(8,128)(2,1)S(1)} %tensor.1), channel_id=1, replica_groups=mesh['z'=8,'ylo'=2,'x'=4,'yhi'=4,'core'=2] {'z','ylo','x'}, dimensions={0} | all-to-all | bytes 1048576 | tf_op jit(solution)/shard_map/all_to_all | solution.py:201
  64.4 0.8 %placed.1 = f32[16,2,128]{2,1,0:T(2,128)} custom-call(bf16[64,32,128]{2,1,0:T(8,128)(2,1)S(1)} %all_to_all.10.refs_0_), custom_call_target="tpu_custom_call" | custom-call | tf_op jit(solution)/shard_map/placed/pallas_call | solution.py:173
  (1 shorter events, 0.0 us)
Async XLA Ops:
  1.7 9.2 %copy-start = (f32[3,16,1024]{2,1,0:T(8,128)S(1)}, f32[3,16,1024]{2,1,0:T(8,128)}, u32[]{:S(2)}) copy-start(f32[3,16,1024]{2,1,0:T(8,128)} %refs_4_.1) | copy-start | bytes 589828
  1.7 16.8 %copy-start.2 = (s32[6,1024]{1,0:T(8,128)S(1)}, s32[6,1024]{1,0:T(8,128)}, u32[]{:S(2)}) copy-start(s32[6,1024]{1,0:T(8,128)} %refs_0_.1) | copy-start | bytes 73732
  1.7 19.2 %all-to-all-start = ((bf16[4,3,16,1024]{3,2,1,0:T(8,128)(2,1)}), bf16[4,3,16,1024]{3,2,1,0:T(8,128)(2,1)S(1)}, u32[]{:S(2)}, u32[]{:S(2)}) async-start(bf16[4,3,16,1024]{3,2,1,0:T(8,128)(2,1)} %broadcast_in_dim.3), calls=%async_computation | async-start | bytes 786432 | tf_op jit(solution)/shard_map/all_to_all | solution.py:189
  11.0 7.5 %copy-start.1 = (f32[3,6,1024]{2,1,0:T(8,128)S(1)}, f32[3,6,1024]{2,1,0:T(8,128)}, u32[]{:S(2)}) copy-start(f32[3,6,1024]{2,1,0:T(8,128)} %refs_1_.1) | copy-start | bytes 221188
  11.0 7.5 %copy-start.3 = (f32[1024]{0:T(1024)S(1)}, f32[1024]{0:T(1024)}, u32[]{:S(2)}) copy-start(f32[1024]{0:T(1024)} %param.6) | copy-start | bytes 12292
  11.0 6.0 %collective-permute-start.1 = (f32[3,16,128]{2,1,0:T(8,128)S(1)}, f32[3,16,128]{2,1,0:T(8,128)S(1)}, u32[]{:S(2)}, u32[]{:S(2)}) collective-permute-start(f32[3,16,128]{2,1,0:T(8,128)S(1)} %get-tuple-element.9), channel_id=1, source_target_pairs={{8,0},{16,8},{24,16},{32,24},{40,32},{48,40},{56,48},{64,56},{72,6... | collective-permute-start | bytes 73736 | tf_op jit(solution)/shard_map/ppermute | solution.py:192
  12.4 6.1 %collective-permute-start = (f32[3,16,128]{2,1,0:T(8,128)S(1)}, f32[3,16,128]{2,1,0:T(8,128)S(1)}, u32[]{:S(2)}, u32[]{:S(2)}) collective-permute-start(f32[3,16,128]{2,1,0:T(8,128)S(1)} %get-tuple-element.10), channel_id=1, source_target_pairs={{0,8},{8,16},{16,24},{24,32},{32,40},{40,48},{48,56},{56,64},{64,7... | collective-permute-start | bytes 73736 | tf_op jit(solution)/shard_map/ppermute | solution.py:191
  20.9 3.6 %collective-permute-start.2 = (bf16[4,3,16,1024]{3,2,1,0:T(8,128)(2,1)S(1)}, bf16[4,3,16,1024]{3,2,1,0:T(8,128)(2,1)S(1)}, u32[]{:S(2)}, u32[]{:S(2)}) collective-permute-start(bf16[4,3,16,1024]{3,2,1,0:T(8,128)(2,1)S(1)} %all-to-all-done.refs_1_), channel_id=1, source_target_pairs={{0,1},{1,0},{2,3},{3,2},{4,5},{5,4},{6,7},{7,6},{8,9},{9,8},{10,11... | collective-permute-start | bytes 1179656 | tf_op jit(solution)/shard_map/ppermute | solution.py:195
